TPU v7x, 32 devices: a whole 2x2x4 slice. The times are simulated.
32 devices in a mesh: group: 2 (over x), area: 16 (over z, y, core).
Axes of the slice: x: 2, y: 2, z: 4, core: 2. Of those that a mesh axis runs over, the one named last changes fastest.
Arguments:
- state_init: float32 [64, 12288], P('group', 'area'), parts along dimension 0, may hold values from -6 to 6
- prior_interval_trace: bfloat16 [4, 64, 12288], P(None, 'group', 'area'), parts along dimension 1, may hold values from -0.8984375 to 0.8984375
- drive_input: bfloat16 [64, 12288], P('group', 'area'), parts along dimension 0, may hold values from -4 to 4
- leak_rate: float32 [24576], P(('group', 'area')), parts along dimension 0, may hold values from 0.15 to 1
- w_recur: bfloat16 [24576, 6144], P(('group', 'area')), parts along dimension 0, may hold values from -0.078125 to 0.078125
- w_send: bfloat16 [24576, 768], P(('group', 'area')), parts along dimension 0, may hold values from -0.078125 to 0.078125
- w_recv: bfloat16 [24576, 768], P(('group', 'area')), parts along dimension 0, may hold values from -0.21875 to 0.21875
- area_mask: int32 [4, 2], P('group'), parts along dimension 0, may hold values 0 or 1
- coupling: float32 [4, 2], P('group'), parts along dimension 0, may hold values from 0.1 to 0.6
- delay_slot: int32 [4, 2], P('group'), parts along dimension 0, may hold values from 0 to 3
Outputs:
- final_state: float32 [64, 12288], P('group', 'area'), parts along dimension 0
- final_history: bfloat16 [4, 64, 12288], P(None, 'group', 'area'), parts along dimension 1
There are 2 independent parts, one for each index of `group`. A program takes and returns all parts, laid end to end along the dimension named above; each array names one. Nothing has to cross between parts.
All inputs are finite; a program needn't handle non-finite values.
Results may differ from a plain program's by a relative error of at most 0.0095.
Values may be sent and summed in bfloat16 or wider, within the bound.
A program may use at most 64 MiB of HBM per device.

v0:
```python
import jax
import jax.numpy as jnp
from jax import lax
from jax.sharding import PartitionSpec as P

SPLIT = 8
INTERVALS = 2


def from_partner(block, axis, bit):
    count = lax.axis_size(axis)
    route = []
    for low in range(count):
        high = low | 1 << bit
        if high != low and high < count:
            route += [(low, high), (high, low)]
    return lax.ppermute(block, axis, route)


def gather_region_activity(spiking_activity):
    device_index = lax.axis_index("area")
    gathered_activity = spiking_activity
    for bit_number in range(SPLIT.bit_length() - 1):
        partner = from_partner(gathered_activity, "area", bit_number)
        upper_half = device_index // 2**bit_number % 2
        gathered_activity = jnp.where(
            upper_half == 1,
            jnp.concatenate([partner, gathered_activity], 1),
            jnp.concatenate([gathered_activity, partner], 1),
        )
    return gathered_activity


def reduce_history(contrib):
    device_index = lax.axis_index("area")
    levels = (lax.axis_size("area") // SPLIT).bit_length() - 1
    for level in reversed(range(levels)):
        half_count = contrib.shape[0] // 2
        upper_half = device_index // (SPLIT * 2**level) % 2
        keeping = jnp.where(upper_half == 1, contrib[half_count:], contrib[:half_count])
        sending = jnp.where(upper_half == 1, contrib[:half_count], contrib[half_count:])
        partner = from_partner(sending, "area", SPLIT.bit_length() - 1 + level)
        contrib = keeping + partner
    return contrib[0]


def body(
    state_init,
    prior_interval_trace,
    drive_input,
    leak_rate,
    w_recur,
    w_send,
    w_recv,
    area_mask,
    coupling,
    delay_slot,
):
    device_index = lax.axis_index("area")
    my_area = device_index // SPLIT
    overall_ticks = prior_interval_trace.shape[0]
    trials_count = prior_interval_trace.shape[1]
    strength = area_mask.astype(jnp.float32) * coupling
    slots = jnp.arange(overall_ticks, dtype=jnp.int32)
    drive = drive_input.astype(jnp.float32)
    part_bits = SPLIT.bit_length() - 1
    neuron_voltage = state_init
    history = prior_interval_trace
    spiking_activity = prior_interval_trace[overall_ticks - 1]
    for interval in range(INTERVALS):
        flat = history.reshape(overall_ticks * trials_count, history.shape[2])
        partial_value = jnp.dot(flat, w_send, preferred_element_type=jnp.float32).reshape(
            overall_ticks, trials_count, w_send.shape[1]
        )
        column = lax.dynamic_index_in_dim(strength, my_area, 1, keepdims=False)
        lagging = lax.dynamic_index_in_dim(delay_slot, my_area, 1, keepdims=False)
        selector = (lagging[:, None] == slots[None, :]).astype(jnp.float32) * column[:, None]
        contrib = jnp.einsum(
            "ak,ktr->atr", selector, partial_value, precision=lax.Precision.HIGHEST
        )
        summed = reduce_history(contrib)
        for bit_number in range(part_bits):
            summed = summed + from_partner(summed, "area", bit_number)
        remote = lax.dot_general(
            summed.astype(jnp.bfloat16),
            w_recv,
            (((1,), (1,)), ((), ())),
            preferred_element_type=jnp.float32,
        )
        logged_activity = []
        for step_index in range(overall_ticks):
            gathered_activity = gather_region_activity(spiking_activity)
            lateral_forcing = lax.dot_general(
                gathered_activity,
                w_recur,
                (((1,), (1,)), ((), ())),
                preferred_element_type=jnp.float32,
            )
            neuron_voltage = neuron_voltage + leak_rate[None, :] * (
                -neuron_voltage + lateral_forcing + remote + drive
            )
            spiking_activity = jnp.tanh(neuron_voltage).astype(jnp.bfloat16)
            logged_activity.append(spiking_activity)
        history = jnp.stack(logged_activity)
    return (neuron_voltage, history)


def solution(mesh):
    in_specs = (
        P("group", "area"),
        P(None, "group", "area"),
        P("group", "area"),
        P(("group", "area")),
        P(("group", "area"), None),
        P(("group", "area"), None),
        P(("group", "area"), None),
        P("group", None),
        P("group", None),
        P("group", None),
    )
    out_specs = (P("group", "area"), P(None, "group", "area"))
    return jax.shard_map(body, mesh=mesh, in_specs=in_specs, out_specs=out_specs, check_vma=False)
```

profile of v0, /device:TPU:0, one launch (start us, length us, event | category | flops | bytes accessed | tf_op | source)
XLA Modules:
  0.0 156.7 jit_solution(16835788837397637880)
XLA Ops:
  4.9 4.1 %collective-permute-start.3 = (f32[1,32,768]{2,0,1:T(1,128)S(1)}, f32[1,32,768]{2,0,1:T(1,128)S(1)}, u32[]{:S(2)}, u32[]{:S(2)}) collective-permute-start(f32[1,32,768]{2,0,1:T(1,128)S(1)} %broadcast_select_fusion.2), channel_id=1, source_target_pairs={{0,8},{8,0},{1,9},{9,1},{2,10},{10,2},{3,11},{11,3},{4,12},{12,4},... | collective-permute-start | bytes 294920 | tf_op jit(solution)/shard_map/ppermute | solution.py:17
  9.0 4.9 %collective-permute-done.3 = f32[1,32,768]{2,0,1:T(1,128)S(1)} collective-permute-done((f32[1,32,768]{2,0,1:T(1,128)S(1)}, f32[1,32,768]{2,0,1:T(1,128)S(1)}, u32[]{:S(2)}, u32[]{:S(2)}) %collective-permute-start.3) | collective-permute-done | bytes 98336 | tf_op jit(solution)/shard_map/ppermute | solution.py:17
  15.5 1.6 %collective-permute-start.5 = (f32[32,768]{1,0:T(8,128)S(1)}, f32[32,768]{1,0:T(8,128)S(1)}, u32[]{:S(2)}, u32[]{:S(2)}) collective-permute-start(f32[32,768]{1,0:T(8,128)S(1)} %fusion.120), channel_id=1, source_target_pairs={{0,2},{2,0},{1,3},{3,1},{4,6},{6,4},{5,7},{7,5},{8,10},{10,8},{9,1... | collective-permute-start | bytes 294920 | tf_op jit(solution)/shard_map/ppermute | solution.py:17
  18.0 3.1 %collective-permute-done.5 = f32[32,768]{1,0:T(8,128)S(1)} collective-permute-done((f32[32,768]{1,0:T(8,128)S(1)}, f32[32,768]{1,0:T(8,128)S(1)}, u32[]{:S(2)}, u32[]{:S(2)}) %collective-permute-start.5) | collective-permute-done | bytes 98336 | tf_op jit(solution)/shard_map/ppermute | solution.py:17
  23.4 3.5 %collective-permute-done.6 = f32[32,768]{1,0:T(8,128)S(1)} collective-permute-done((f32[32,768]{1,0:T(8,128)S(1)}, f32[32,768]{1,0:T(8,128)S(1)}, u32[]{:S(2)}, u32[]{:S(2)}) %collective-permute-start.6) | collective-permute-done | bytes 98336 | tf_op jit(solution)/shard_map/ppermute | solution.py:17
  26.9 1.7 %fusion.97 = f32[32,768]{1,0:T(8,128)S(1)} fusion(bf16[768,768]{1,0:T(8,128)(2,1)} %param.16, f32[32,768]{1,0:T(8,128)S(1)} %add.175, f32[32,768]{1,0:T(8,128)S(1)} %collective-permute-done.6), kind=kOutput, calls=%fused_computation.146 | convolution fusion | flops 37797888 | bytes 1474560 | tf_op jit(solution)/shard_map/dot_general | solution.py:84
  29.9 6.7 %tanh_convert_fusion.7 = (bf16[32,768]{1,0:T(8,128)(2,1)S(1)}, f32[32,768]{1,0:T(8,128)S(1)}) fusion(f32[32,768]{1,0:T(8,128)} %param.10, bf16[32,768]{1,0:T(8,128)(2,1)} %param.12, f32[32,768]{1,0:T(8,128)S(1)} %fusion.97, bf16[768,6144]{1,0:T(8,128)(2,1)} %param.14, bf16[32,3072]{1,0:T(8,128)(2,1)S(1)} %maximum_select_fusion.16, ...), kind=kOutput, calls=%fused_computation.144 | convolution fusion | flops 303955968 | bytes 10226689 | tf_op jit(solution)/shard_map/dot_general | solution.py:93
  37.9 1.5 collective-permute-start.8
  39.4 3.4 %collective-permute-done.8 = bf16[32,1536]{1,0:T(8,128)(2,1)S(1)} collective-permute-done((bf16[32,1536]{1,0:T(8,128)(2,1)S(1)}, bf16[32,1536]{1,0:T(8,128)(2,1)S(1)}, u32[]{:S(2)}, u32[]{:S(2)}) %collective-permute-start.8) | collective-permute-done | bytes 98336 | tf_op jit(solution)/shard_map/ppermute | solution.py:17
  43.6 5.4 %collective-permute-done.9 = bf16[32,3072]{1,0:T(8,128)(2,1)S(1)} collective-permute-done((bf16[32,3072]{1,0:T(8,128)(2,1)S(1)}, bf16[32,3072]{1,0:T(8,128)(2,1)S(1)}, u32[]{:S(2)}, u32[]{:S(2)}) %collective-permute-start.9) | collective-permute-done | bytes 196640 | tf_op jit(solution)/shard_map/ppermute | solution.py:17
  49.0 2.9 %tanh_convert_fusion.6 = (bf16[32,768]{1,0:T(8,128)(2,1)S(1)}, f32[32,768]{1,0:T(8,128)S(1)}) fusion(f32[32,768]{1,0:T(8,128)S(1)} %get-tuple-element.3, bf16[32,768]{1,0:T(8,128)(2,1)S(1)} %copy-done.3, f32[32,768]{1,0:T(8,128)S(1)} %fusion.97, bf16[768,6144]{1,0:T(8,128)(2,1)S(1)} %copy-done.1, bf16[32,3072]{1,0:T(8,128)(2,1)S(1)} %maximum_select_fusion.17, ...), kind=kOutput, calls=%fused_computation.143 | convolution fusion | flops 303955968 | bytes 10226689 | tf_op jit(solution)/shard_map/dot_general | solution.py:93
  54.8 3.4 %collective-permute-done.11 = bf16[32,1536]{1,0:T(8,128)(2,1)S(1)} collective-permute-done((bf16[32,1536]{1,0:T(8,128)(2,1)S(1)}, bf16[32,1536]{1,0:T(8,128)(2,1)S(1)}, u32[]{:S(2)}, u32[]{:S(2)}) %collective-permute-start.11) | collective-permute-done | bytes 98336 | tf_op jit(solution)/shard_map/ppermute | solution.py:17
  59.0 5.4 %collective-permute-done.12 = bf16[32,3072]{1,0:T(8,128)(2,1)S(1)} collective-permute-done((bf16[32,3072]{1,0:T(8,128)(2,1)S(1)}, bf16[32,3072]{1,0:T(8,128)(2,1)S(1)}, u32[]{:S(2)}, u32[]{:S(2)}) %collective-permute-start.12) | collective-permute-done | bytes 196640 | tf_op jit(solution)/shard_map/ppermute | solution.py:17
  64.4 2.9 %tanh_convert_fusion.5 = (bf16[32,768]{1,0:T(8,128)(2,1)S(1)}, f32[32,768]{1,0:T(8,128)S(1)}) fusion(f32[32,768]{1,0:T(8,128)S(1)} %get-tuple-element.5, bf16[32,768]{1,0:T(8,128)(2,1)S(1)} %copy-done.3, f32[32,768]{1,0:T(8,128)S(1)} %fusion.97, bf16[768,6144]{1,0:T(8,128)(2,1)S(1)} %copy-done.1, bf16[32,3072]{1,0:T(8,128)(2,1)S(1)} %maximum_select_fusion.18, ...), kind=kOutput, calls=%fused_computation.142 | convolution fusion | flops 303955968 | bytes 10226689 | tf_op jit(solution)/shard_map/dot_general | solution.py:93
  70.2 3.4 %collective-permute-done.14 = bf16[32,1536]{1,0:T(8,128)(2,1)S(1)} collective-permute-done((bf16[32,1536]{1,0:T(8,128)(2,1)S(1)}, bf16[32,1536]{1,0:T(8,128)(2,1)S(1)}, u32[]{:S(2)}, u32[]{:S(2)}) %collective-permute-start.14) | collective-permute-done | bytes 98336 | tf_op jit(solution)/shard_map/ppermute | solution.py:17
  74.4 5.4 %collective-permute-done.15 = bf16[32,3072]{1,0:T(8,128)(2,1)S(1)} collective-permute-done((bf16[32,3072]{1,0:T(8,128)(2,1)S(1)}, bf16[32,3072]{1,0:T(8,128)(2,1)S(1)}, u32[]{:S(2)}, u32[]{:S(2)}) %collective-permute-start.15) | collective-permute-done | bytes 196640 | tf_op jit(solution)/shard_map/ppermute | solution.py:17
  79.9 2.9 %tanh_convert_fusion.4 = (bf16[32,768]{1,0:T(8,128)(2,1)S(1)}, f32[32,768]{1,0:T(8,128)S(1)}) fusion(f32[32,768]{1,0:T(8,128)S(1)} %get-tuple-element.7, bf16[32,768]{1,0:T(8,128)(2,1)S(1)} %copy-done.3, f32[32,768]{1,0:T(8,128)S(1)} %fusion.97, bf16[768,6144]{1,0:T(8,128)(2,1)S(1)} %copy-done.1, bf16[32,3072]{1,0:T(8,128)(2,1)S(1)} %maximum_select_fusion.19, ...), kind=kOutput, calls=%fused_computation.141 | convolution fusion | flops 303955968 | bytes 10226689 | tf_op jit(solution)/shard_map/dot_general | solution.py:93
  84.4 2.4 %collective-permute-start.19 = (f32[1,32,768]{2,0,1:T(1,128)S(1)}, f32[1,32,768]{2,0,1:T(1,128)S(1)}, u32[]{:S(2)}, u32[]{:S(2)}) collective-permute-start(f32[1,32,768]{2,0,1:T(1,128)S(1)} %broadcast_select_fusion), channel_id=1, source_target_pairs={{0,8},{8,0},{1,9},{9,1},{2,10},{10,2},{3,11},{11,3},{4,12},{12,4},... | collective-permute-start | bytes 294920 | tf_op jit(solution)/shard_map/ppermute | solution.py:17
  86.8 4.3 %collective-permute-done.19 = f32[1,32,768]{2,0,1:T(1,128)S(1)} collective-permute-done((f32[1,32,768]{2,0,1:T(1,128)S(1)}, f32[1,32,768]{2,0,1:T(1,128)S(1)}, u32[]{:S(2)}, u32[]{:S(2)}) %collective-permute-start.19) | collective-permute-done | bytes 98336 | tf_op jit(solution)/shard_map/ppermute | solution.py:17
  94.8 3.5 %collective-permute-done.21 = f32[32,768]{1,0:T(8,128)S(1)} collective-permute-done((f32[32,768]{1,0:T(8,128)S(1)}, f32[32,768]{1,0:T(8,128)S(1)}, u32[]{:S(2)}, u32[]{:S(2)}) %collective-permute-start.21) | collective-permute-done | bytes 98336 | tf_op jit(solution)/shard_map/ppermute | solution.py:17
  100.5 3.5 %collective-permute-done.22 = f32[32,768]{1,0:T(8,128)S(1)} collective-permute-done((f32[32,768]{1,0:T(8,128)S(1)}, f32[32,768]{1,0:T(8,128)S(1)}, u32[]{:S(2)}, u32[]{:S(2)}) %collective-permute-start.22) | collective-permute-done | bytes 98336 | tf_op jit(solution)/shard_map/ppermute | solution.py:17
  104.5 2.3 %collective-permute-done.18 = bf16[32,3072]{1,0:T(8,128)(2,1)S(1)} collective-permute-done((bf16[32,3072]{1,0:T(8,128)(2,1)S(1)}, bf16[32,3072]{1,0:T(8,128)(2,1)S(1)}, u32[]{:S(2)}, u32[]{:S(2)}) %collective-permute-start.18) | collective-permute-done | bytes 196640 | tf_op jit(solution)/shard_map/ppermute | solution.py:17
  106.9 2.9 %tanh_convert_fusion.3 = (bf16[32,768]{1,0:T(8,128)(2,1)S(1)}, f32[32,768]{1,0:T(8,128)S(1)}) fusion(f32[32,768]{1,0:T(8,128)S(1)} %get-tuple-element.9, bf16[32,768]{1,0:T(8,128)(2,1)S(1)} %copy-done.3, f32[32,768]{1,0:T(8,128)S(1)} %fusion.98, bf16[768,6144]{1,0:T(8,128)(2,1)S(1)} %copy-done.1, bf16[32,3072]{1,0:T(8,128)(2,1)S(1)} %maximum_select_fusion.20, ...), kind=kOutput, calls=%fused_computation.139 | convolution fusion | flops 303955968 | bytes 10226689 | tf_op jit(solution)/shard_map/dot_general | solution.py:93
  112.6 3.4 %collective-permute-done.24 = bf16[32,1536]{1,0:T(8,128)(2,1)S(1)} collective-permute-done((bf16[32,1536]{1,0:T(8,128)(2,1)S(1)}, bf16[32,1536]{1,0:T(8,128)(2,1)S(1)}, u32[]{:S(2)}, u32[]{:S(2)}) %collective-permute-start.24) | collective-permute-done | bytes 98336 | tf_op jit(solution)/shard_map/ppermute | solution.py:17
  116.5 5.7 %collective-permute-done.25 = bf16[32,3072]{1,0:T(8,128)(2,1)S(1)} collective-permute-done((bf16[32,3072]{1,0:T(8,128)(2,1)S(1)}, bf16[32,3072]{1,0:T(8,128)(2,1)S(1)}, u32[]{:S(2)}, u32[]{:S(2)}) %collective-permute-start.25) | collective-permute-done | bytes 196640 | tf_op jit(solution)/shard_map/ppermute | solution.py:17
  122.3 2.9 %tanh_convert_fusion.2 = (bf16[32,768]{1,0:T(8,128)(2,1)S(1)}, f32[32,768]{1,0:T(8,128)S(1)}) fusion(f32[32,768]{1,0:T(8,128)S(1)} %get-tuple-element.11, bf16[32,768]{1,0:T(8,128)(2,1)S(1)} %copy-done.3, f32[32,768]{1,0:T(8,128)S(1)} %fusion.98, bf16[768,6144]{1,0:T(8,128)(2,1)S(1)} %copy-done.1, bf16[32,3072]{1,0:T(8,128)(2,1)S(1)} %maximum_select_fusion.21, ...), kind=kOutput, calls=%fused_computation.138 | convolution fusion | flops 303955968 | bytes 10226689 | tf_op jit(solution)/shard_map/dot_general | solution.py:93
  128.0 3.4 %collective-permute-done.27 = bf16[32,1536]{1,0:T(8,128)(2,1)S(1)} collective-permute-done((bf16[32,1536]{1,0:T(8,128)(2,1)S(1)}, bf16[32,1536]{1,0:T(8,128)(2,1)S(1)}, u32[]{:S(2)}, u32[]{:S(2)}) %collective-permute-start.27) | collective-permute-done | bytes 98336 | tf_op jit(solution)/shard_map/ppermute | solution.py:17
  131.9 5.7 %collective-permute-done.28 = bf16[32,3072]{1,0:T(8,128)(2,1)S(1)} collective-permute-done((bf16[32,3072]{1,0:T(8,128)(2,1)S(1)}, bf16[32,3072]{1,0:T(8,128)(2,1)S(1)}, u32[]{:S(2)}, u32[]{:S(2)}) %collective-permute-start.28) | collective-permute-done | bytes 196640 | tf_op jit(solution)/shard_map/ppermute | solution.py:17
  137.7 2.9 %tanh_convert_fusion.1 = (bf16[32,768]{1,0:T(8,128)(2,1)S(1)}, f32[32,768]{1,0:T(8,128)S(1)}) fusion(f32[32,768]{1,0:T(8,128)S(1)} %get-tuple-element.13, bf16[32,768]{1,0:T(8,128)(2,1)S(1)} %copy-done.3, f32[32,768]{1,0:T(8,128)S(1)} %fusion.98, bf16[768,6144]{1,0:T(8,128)(2,1)S(1)} %copy-done.1, bf16[32,3072]{1,0:T(8,128)(2,1)S(1)} %maximum_select_fusion.22, ...), kind=kOutput, calls=%fused_computation.137 | convolution fusion | flops 303955968 | bytes 10226689 | tf_op jit(solution)/shard_map/dot_general | solution.py:93
  143.4 3.4 %collective-permute-done.30 = bf16[32,1536]{1,0:T(8,128)(2,1)S(1)} collective-permute-done((bf16[32,1536]{1,0:T(8,128)(2,1)S(1)}, bf16[32,1536]{1,0:T(8,128)(2,1)S(1)}, u32[]{:S(2)}, u32[]{:S(2)}) %collective-permute-start.30) | collective-permute-done | bytes 98336 | tf_op jit(solution)/shard_map/ppermute | solution.py:17
  147.3 5.7 %collective-permute-done.31 = bf16[32,3072]{1,0:T(8,128)(2,1)S(1)} collective-permute-done((bf16[32,3072]{1,0:T(8,128)(2,1)S(1)}, bf16[32,3072]{1,0:T(8,128)(2,1)S(1)}, u32[]{:S(2)}, u32[]{:S(2)}) %collective-permute-start.31) | collective-permute-done | bytes 196640 | tf_op jit(solution)/shard_map/ppermute | solution.py:17
  153.1 2.9 %fusion.7 = f32[32,768]{1,0:T(8,128)S(1)} fusion(f32[32,768]{1,0:T(8,128)S(1)} %get-tuple-element.15, f32[32,768]{1,0:T(8,128)S(1)} %fusion.98, bf16[768,6144]{1,0:T(8,128)(2,1)S(1)} %copy-done.1, bf16[32,3072]{1,0:T(8,128)(2,1)S(1)} %maximum_select_fusion.23, bf16[32,3072]{1,0:T(8,128)(2,1)S(1)} %collective-permute-done.31, pred[]{:T(512)S(6)} %eq.43, ...), kind=kOutput, calls=%fused_computation.8 | convolution fusion | flops 303931392 | bytes 10177537 | tf_op jit(solution)/shard_map/dot_general | solution.py:93
  (90 shorter events, 38.1 us)
Async XLA Ops:
  4.9 9.0 %collective-permute-start.3 = (f32[1,32,768]{2,0,1:T(1,128)S(1)}, f32[1,32,768]{2,0,1:T(1,128)S(1)}, u32[]{:S(2)}, u32[]{:S(2)}) collective-permute-start(f32[1,32,768]{2,0,1:T(1,128)S(1)} %broadcast_select_fusion.2), channel_id=1, source_target_pairs={{0,8},{8,0},{1,9},{9,1},{2,10},{10,2},{3,11},{11,3},{4,12},{12,4},... | collective-permute-start | bytes 294920 | tf_op jit(solution)/shard_map/ppermute | solution.py:17
  14.1 1.4 collective-permute-start.4
  15.0 2.2 %collective-permute-start = (bf16[32,768]{1,0:T(8,128)(2,1)S(1)}, bf16[32,768]{1,0:T(8,128)(2,1)S(1)}, u32[]{:S(2)}, u32[]{:S(2)}) collective-permute-start(bf16[32,768]{1,0:T(8,128)(2,1)S(1)} %slice_bitcast_fusion), channel_id=1, source_target_pairs={{0,1},{1,0},{2,3},{3,2},{4,5},{5,4},{6,7},{7,6},{8,9},{9,8},{10,11... | collective-permute-start | bytes 147464 | tf_op jit(solution)/shard_map/ppermute | solution.py:17
  15.5 5.6 %collective-permute-start.5 = (f32[32,768]{1,0:T(8,128)S(1)}, f32[32,768]{1,0:T(8,128)S(1)}, u32[]{:S(2)}, u32[]{:S(2)}) collective-permute-start(f32[32,768]{1,0:T(8,128)S(1)} %fusion.120), channel_id=1, source_target_pairs={{0,2},{2,0},{1,3},{3,1},{4,6},{6,4},{5,7},{7,5},{8,10},{10,8},{9,1... | collective-permute-start | bytes 294920 | tf_op jit(solution)/shard_map/ppermute | solution.py:17
  17.2 5.3 %collective-permute-start.1 = (bf16[32,1536]{1,0:T(8,128)(2,1)S(1)}, bf16[32,1536]{1,0:T(8,128)(2,1)S(1)}, u32[]{:S(2)}, u32[]{:S(2)}) collective-permute-start(bf16[32,1536]{1,0:T(8,128)(2,1)S(1)} %maximum_select_fusion.24), channel_id=1, source_target_pairs={{0,2},{2,0},{1,3},{3,1},{4,6},{6,4},{5,7},{7,5},{8,10},{10,8},{9,1... | collective-permute-start | bytes 294920 | tf_op jit(solution)/shard_map/ppermute | solution.py:17
  21.2 5.7 %collective-permute-start.6 = (f32[32,768]{1,0:T(8,128)S(1)}, f32[32,768]{1,0:T(8,128)S(1)}, u32[]{:S(2)}, u32[]{:S(2)}) collective-permute-start(f32[32,768]{1,0:T(8,128)S(1)} %add.175), channel_id=1, source_target_pairs={{0,4},{4,0},{1,5},{5,1},{2,6},{6,2},{3,7},{7,3},{8,12},{12,8},{9,1... | collective-permute-start | bytes 294920 | tf_op jit(solution)/shard_map/ppermute | solution.py:17
  22.6 7.3 %collective-permute-start.2 = (bf16[32,3072]{1,0:T(8,128)(2,1)S(1)}, bf16[32,3072]{1,0:T(8,128)(2,1)S(1)}, u32[]{:S(2)}, u32[]{:S(2)}) collective-permute-start(bf16[32,3072]{1,0:T(8,128)(2,1)S(1)} %maximum_select_fusion.16), channel_id=1, source_target_pairs={{0,4},{4,0},{1,5},{5,1},{2,6},{6,2},{3,7},{7,3},{8,12},{12,8},{9,1... | collective-permute-start | bytes 589832 | tf_op jit(solution)/shard_map/ppermute | solution.py:17
  36.6 1.3 collective-permute-start.7
  37.9 4.9 %collective-permute-start.8 = (bf16[32,1536]{1,0:T(8,128)(2,1)S(1)}, bf16[32,1536]{1,0:T(8,128)(2,1)S(1)}, u32[]{:S(2)}, u32[]{:S(2)}) collective-permute-start(bf16[32,1536]{1,0:T(8,128)(2,1)S(1)} %maximum_select_fusion.25), channel_id=1, source_target_pairs={{0,2},{2,0},{1,3},{3,1},{4,6},{6,4},{5,7},{7,5},{8,10},{10,8},{9,1... | collective-permute-start | bytes 294920 | tf_op jit(solution)/shard_map/ppermute | solution.py:17
  42.9 6.2 %collective-permute-start.9 = (bf16[32,3072]{1,0:T(8,128)(2,1)S(1)}, bf16[32,3072]{1,0:T(8,128)(2,1)S(1)}, u32[]{:S(2)}, u32[]{:S(2)}) collective-permute-start(bf16[32,3072]{1,0:T(8,128)(2,1)S(1)} %maximum_select_fusion.17), channel_id=1, source_target_pairs={{0,4},{4,0},{1,5},{5,1},{2,6},{6,2},{3,7},{7,3},{8,12},{12,8},{9,1... | collective-permute-start | bytes 589832 | tf_op jit(solution)/shard_map/ppermute | solution.py:17
  52.0 1.3 collective-permute-start.10
  53.3 4.9 %collective-permute-start.11 = (bf16[32,1536]{1,0:T(8,128)(2,1)S(1)}, bf16[32,1536]{1,0:T(8,128)(2,1)S(1)}, u32[]{:S(2)}, u32[]{:S(2)}) collective-permute-start(bf16[32,1536]{1,0:T(8,128)(2,1)S(1)} %maximum_select_fusion.26), channel_id=1, source_target_pairs={{0,2},{2,0},{1,3},{3,1},{4,6},{6,4},{5,7},{7,5},{8,10},{10,8},{9,1... | collective-permute-start | bytes 294920 | tf_op jit(solution)/shard_map/ppermute | solution.py:17
  58.3 6.2 %collective-permute-start.12 = (bf16[32,3072]{1,0:T(8,128)(2,1)S(1)}, bf16[32,3072]{1,0:T(8,128)(2,1)S(1)}, u32[]{:S(2)}, u32[]{:S(2)}) collective-permute-start(bf16[32,3072]{1,0:T(8,128)(2,1)S(1)} %maximum_select_fusion.18), channel_id=1, source_target_pairs={{0,4},{4,0},{1,5},{5,1},{2,6},{6,2},{3,7},{7,3},{8,12},{12,8},{9,1... | collective-permute-start | bytes 589832 | tf_op jit(solution)/shard_map/ppermute | solution.py:17
  67.4 1.3 collective-permute-start.13
  68.7 4.9 %collective-permute-start.14 = (bf16[32,1536]{1,0:T(8,128)(2,1)S(1)}, bf16[32,1536]{1,0:T(8,128)(2,1)S(1)}, u32[]{:S(2)}, u32[]{:S(2)}) collective-permute-start(bf16[32,1536]{1,0:T(8,128)(2,1)S(1)} %maximum_select_fusion.27), channel_id=1, source_target_pairs={{0,2},{2,0},{1,3},{3,1},{4,6},{6,4},{5,7},{7,5},{8,10},{10,8},{9,1... | collective-permute-start | bytes 294920 | tf_op jit(solution)/shard_map/ppermute | solution.py:17
  73.7 6.2 %collective-permute-start.15 = (bf16[32,3072]{1,0:T(8,128)(2,1)S(1)}, bf16[32,3072]{1,0:T(8,128)(2,1)S(1)}, u32[]{:S(2)}, u32[]{:S(2)}) collective-permute-start(bf16[32,3072]{1,0:T(8,128)(2,1)S(1)} %maximum_select_fusion.19), channel_id=1, source_target_pairs={{0,4},{4,0},{1,5},{5,1},{2,6},{6,2},{3,7},{7,3},{8,12},{12,8},{9,1... | collective-permute-start | bytes 589832 | tf_op jit(solution)/shard_map/ppermute | solution.py:17
  84.4 6.6 %collective-permute-start.19 = (f32[1,32,768]{2,0,1:T(1,128)S(1)}, f32[1,32,768]{2,0,1:T(1,128)S(1)}, u32[]{:S(2)}, u32[]{:S(2)}) collective-permute-start(f32[1,32,768]{2,0,1:T(1,128)S(1)} %broadcast_select_fusion), channel_id=1, source_target_pairs={{0,8},{8,0},{1,9},{9,1},{2,10},{10,2},{3,11},{11,3},{4,12},{12,4},... | collective-permute-start | bytes 294920 | tf_op jit(solution)/shard_map/ppermute | solution.py:17
  91.2 1.4 collective-permute-start.20
  91.3 2.8 %collective-permute-start.16 = (bf16[32,768]{1,0:T(8,128)(2,1)S(1)}, bf16[32,768]{1,0:T(8,128)(2,1)S(1)}, u32[]{:S(2)}, u32[]{:S(2)}) collective-permute-start(bf16[32,768]{1,0:T(8,128)(2,1)S(1)} %get-tuple-element.8), channel_id=1, source_target_pairs={{0,1},{1,0},{2,3},{3,2},{4,5},{5,4},{6,7},{7,6},{8,9},{9,8},{10,11... | collective-permute-start | bytes 147464 | tf_op jit(solution)/shard_map/ppermute | solution.py:17
  92.6 5.7 %collective-permute-start.21 = (f32[32,768]{1,0:T(8,128)S(1)}, f32[32,768]{1,0:T(8,128)S(1)}, u32[]{:S(2)}, u32[]{:S(2)}) collective-permute-start(f32[32,768]{1,0:T(8,128)S(1)} %fusion.121), channel_id=1, source_target_pairs={{0,2},{2,0},{1,3},{3,1},{4,6},{6,4},{5,7},{7,5},{8,10},{10,8},{9,1... | collective-permute-start | bytes 294920 | tf_op jit(solution)/shard_map/ppermute | solution.py:17
  94.1 5.5 %collective-permute-start.17 = (bf16[32,1536]{1,0:T(8,128)(2,1)S(1)}, bf16[32,1536]{1,0:T(8,128)(2,1)S(1)}, u32[]{:S(2)}, u32[]{:S(2)}) collective-permute-start(bf16[32,1536]{1,0:T(8,128)(2,1)S(1)} %maximum_select_fusion.28), channel_id=1, source_target_pairs={{0,2},{2,0},{1,3},{3,1},{4,6},{6,4},{5,7},{7,5},{8,10},{10,8},{9,1... | collective-permute-start | bytes 294920 | tf_op jit(solution)/shard_map/ppermute | solution.py:17
  98.3 5.7 %collective-permute-start.22 = (f32[32,768]{1,0:T(8,128)S(1)}, f32[32,768]{1,0:T(8,128)S(1)}, u32[]{:S(2)}, u32[]{:S(2)}) collective-permute-start(f32[32,768]{1,0:T(8,128)S(1)} %add.195), channel_id=1, source_target_pairs={{0,4},{4,0},{1,5},{5,1},{2,6},{6,2},{3,7},{7,3},{8,12},{12,8},{9,1... | collective-permute-start | bytes 294920 | tf_op jit(solution)/shard_map/ppermute | solution.py:17
  99.7 7.2 %collective-permute-start.18 = (bf16[32,3072]{1,0:T(8,128)(2,1)S(1)}, bf16[32,3072]{1,0:T(8,128)(2,1)S(1)}, u32[]{:S(2)}, u32[]{:S(2)}) collective-permute-start(bf16[32,3072]{1,0:T(8,128)(2,1)S(1)} %maximum_select_fusion.20), channel_id=1, source_target_pairs={{0,4},{4,0},{1,5},{5,1},{2,6},{6,2},{3,7},{7,3},{8,12},{12,8},{9,1... | collective-permute-start | bytes 589832 | tf_op jit(solution)/shard_map/ppermute | solution.py:17
  109.8 1.3 collective-permute-start.23
  111.1 4.9 %collective-permute-start.24 = (bf16[32,1536]{1,0:T(8,128)(2,1)S(1)}, bf16[32,1536]{1,0:T(8,128)(2,1)S(1)}, u32[]{:S(2)}, u32[]{:S(2)}) collective-permute-start(bf16[32,1536]{1,0:T(8,128)(2,1)S(1)} %maximum_select_fusion.29), channel_id=1, source_target_pairs={{0,2},{2,0},{1,3},{3,1},{4,6},{6,4},{5,7},{7,5},{8,10},{10,8},{9,1... | collective-permute-start | bytes 294920 | tf_op jit(solution)/shard_map/ppermute | solution.py:17
  116.1 6.2 %collective-permute-start.25 = (bf16[32,3072]{1,0:T(8,128)(2,1)S(1)}, bf16[32,3072]{1,0:T(8,128)(2,1)S(1)}, u32[]{:S(2)}, u32[]{:S(2)}) collective-permute-start(bf16[32,3072]{1,0:T(8,128)(2,1)S(1)} %maximum_select_fusion.21), channel_id=1, source_target_pairs={{0,4},{4,0},{1,5},{5,1},{2,6},{6,2},{3,7},{7,3},{8,12},{12,8},{9,1... | collective-permute-start | bytes 589832 | tf_op jit(solution)/shard_map/ppermute | solution.py:17
  125.2 1.3 collective-permute-start.26
  126.5 4.9 %collective-permute-start.27 = (bf16[32,1536]{1,0:T(8,128)(2,1)S(1)}, bf16[32,1536]{1,0:T(8,128)(2,1)S(1)}, u32[]{:S(2)}, u32[]{:S(2)}) collective-permute-start(bf16[32,1536]{1,0:T(8,128)(2,1)S(1)} %maximum_select_fusion.30), channel_id=1, source_target_pairs={{0,2},{2,0},{1,3},{3,1},{4,6},{6,4},{5,7},{7,5},{8,10},{10,8},{9,1... | collective-permute-start | bytes 294920 | tf_op jit(solution)/shard_map/ppermute | solution.py:17
  131.5 6.2 %collective-permute-start.28 = (bf16[32,3072]{1,0:T(8,128)(2,1)S(1)}, bf16[32,3072]{1,0:T(8,128)(2,1)S(1)}, u32[]{:S(2)}, u32[]{:S(2)}) collective-permute-start(bf16[32,3072]{1,0:T(8,128)(2,1)S(1)} %maximum_select_fusion.22), channel_id=1, source_target_pairs={{0,4},{4,0},{1,5},{5,1},{2,6},{6,2},{3,7},{7,3},{8,12},{12,8},{9,1... | collective-permute-start | bytes 589832 | tf_op jit(solution)/shard_map/ppermute | solution.py:17
  140.6 1.3 collective-permute-start.29
  141.9 4.9 %collective-permute-start.30 = (bf16[32,1536]{1,0:T(8,128)(2,1)S(1)}, bf16[32,1536]{1,0:T(8,128)(2,1)S(1)}, u32[]{:S(2)}, u32[]{:S(2)}) collective-permute-start(bf16[32,1536]{1,0:T(8,128)(2,1)S(1)} %maximum_select_fusion.31), channel_id=1, source_target_pairs={{0,2},{2,0},{1,3},{3,1},{4,6},{6,4},{5,7},{7,5},{8,10},{10,8},{9,1... | collective-permute-start | bytes 294920 | tf_op jit(solution)/shard_map/ppermute | solution.py:17
  146.9 6.2 %collective-permute-start.31 = (bf16[32,3072]{1,0:T(8,128)(2,1)S(1)}, bf16[32,3072]{1,0:T(8,128)(2,1)S(1)}, u32[]{:S(2)}, u32[]{:S(2)}) collective-permute-start(bf16[32,3072]{1,0:T(8,128)(2,1)S(1)} %maximum_select_fusion.23), channel_id=1, source_target_pairs={{0,4},{4,0},{1,5},{5,1},{2,6},{6,2},{3,7},{7,3},{8,12},{12,8},{9,1... | collective-permute-start | bytes 589832 | tf_op jit(solution)/shard_map/ppermute | solution.py:17
  (6 other events, 167.1 us)
where the time goes:
time: 157 us
  waiting for transfers between devices  89.8 us (57%)
  matrix products  33 us (21%)
  starting transfers between devices  28.4 us (18%)
  other arithmetic  2.62 us (2%)
  local copies, waits for them, and re-layouts  1.91 us (1%)
    ppermute x32, waiting for transfers between devices, from_partner(): return lax.ppermute(block, axis, route)  89.8 us
    ppermute x32, starting transfers between devices, from_partner(): return lax.ppermute(block, axis, route)  28.4 us
    dot_general x8, matrix products, body(): lax.dot_general(gathered_activity, w_recur, (((1,), (1,)), ((), ())), pre...  27.1 us
  transfers between devices with their start and end apart: 32, of which 29 were waited for; matrix products, arithmetic and copies ran while one was open for 2% of the time, Pallas kernels for 0%

commit v1 on v0

v1 whole, which is shorter than its diff:
```python
import functools

import jax
import jax.numpy as jnp
from jax import lax
from jax.experimental import pallas as pl
from jax.experimental.pallas import tpu as pltpu
from jax.sharding import PartitionSpec as P

INTERVALS = 2
TRANSPOSED = (((1,), (1,)), ((), ()))


def flip(index, mask):
    bit = 1
    while bit <= mask:
        if mask & bit:
            index = index + bit - 2 * bit * ((index // bit) % 2)
        bit *= 2
    return index


def kernel(
    devices, split, state, prior, drive, leak, w_recur, w_send, w_recv, mask, coupling, delay,
    voltage, history,
    w_rec, w_snd, w_rcv, rates, readout, outgoing, incoming, subspace, base,
    w_sem, send_sem, fwd_sem, recv_sem, out_sem, in_sem, sub_send, sub_recv,
):
    me = lax.axis_index("area")
    place = me % split
    area = me // split
    areas = devices // split
    ticks, trials, units = prior.shape
    rows = trials // split
    forwarded = range(2, split, 2)

    def load_recur(m):
        start = pl.multiple_of(flip(place, m) * units, units)
        return pltpu.make_async_copy(w_recur.at[:, pl.ds(start, units)], w_rec.at[m], w_sem.at[m])

    load_send = pltpu.make_async_copy(w_send, w_snd, w_sem.at[split])
    load_recv = pltpu.make_async_copy(w_recv, w_rcv, w_sem.at[split + 1])

    load_send.start()
    for m in range(split):
        load_recur(m).start()
    load_recv.start()

    barrier = pltpu.get_barrier_semaphore()

    @pl.loop(1, devices)
    def _(o):
        pl.semaphore_signal(barrier, inc=1, device_id={"area": (me + o) % devices})

    voltage[...] = state[...]
    rates[0, 0] = prior[ticks - 1]
    load_send.wait()
    for k in range(ticks - 1):
        readout[k] = jnp.dot(prior[k], w_snd[...], preferred_element_type=jnp.float32)
    pl.semaphore_wait(barrier, devices - 1)

    def rate_copy(par, m):
        return pltpu.make_async_remote_copy(
            src_ref=rates.at[par, 0], dst_ref=rates.at[par, m],
            send_sem=send_sem.at[m], recv_sem=recv_sem.at[par, m],
            device_id={"area": flip(me, m)},
        )

    def rate_forward(par, m):
        return pltpu.make_async_remote_copy(
            src_ref=rates.at[par, m], dst_ref=rates.at[par, m + 1],
            send_sem=fwd_sem.at[m], recv_sem=recv_sem.at[par, m + 1],
            device_id={"area": flip(me, 1)},
        )

    def part_copy(it, o):
        target = (me + o) % devices
        return pltpu.make_async_remote_copy(
            src_ref=outgoing.at[target // split, target % split], dst_ref=incoming.at[it, o],
            send_sem=out_sem.at[o], recv_sem=in_sem.at[it, o],
            device_id={"area": target},
        )

    def sub_copy(it, m):
        return pltpu.make_async_remote_copy(
            src_ref=subspace.at[it, place], dst_ref=subspace.at[it, place],
            send_sem=sub_send.at[m], recv_sem=sub_recv.at[it, m],
            device_id={"area": flip(me, m)},
        )

    def matmul(par, m):
        return lax.dot_general(rates[par, m], w_rec[m], TRANSPOSED, preferred_element_type=jnp.float32)

    def step(it, k, first):
        par = (it * ticks + k) % 2

        def ready(m):
            if first:
                @pl.when(it == 0)
                def _():
                    load_recur(m).wait()

        for m in reversed(forwarded):
            rate_copy(par, m).start()
        rate_copy(par, 1).start()
        readout[(k + ticks - 1) % ticks] = jnp.dot(
            rates[par, 0], w_snd[...], preferred_element_type=jnp.float32
        )
        if first:
            for a in range(areas):
                strength = mask[a, area].astype(jnp.float32) * coupling[a, area]
                part = readout[delay[a, area]] * strength
                for j in range(split):
                    outgoing[a, j] = part[j * rows : (j + 1) * rows]

            @pl.loop(1, devices)
            def _(o):
                part_copy(it, o).start()

        ready(0)
        acc = matmul(par, 0)
        if not first:
            acc = acc + base[...]
        rate_copy(par, 1).wait_recv()
        ready(1)
        acc = acc + matmul(par, 1)
        *early, late = forwarded
        for m in early:
            rate_copy(par, m).wait_recv()
            rate_forward(par, m).start()
        for m in early:
            ready(m)
            acc = acc + matmul(par, m)
        rate_copy(par, late).wait_recv()
        rate_forward(par, late).start()
        if first:
            def add(o, total):
                part_copy(it, o).wait_recv()
                return total + incoming[it, o]

            subspace[it, place] = lax.fori_loop(1, devices, add, outgoing[area, place])
            for m in range(1, split):
                sub_copy(it, m).start()
        for m in early:
            rate_forward(par, m).wait_recv()
            ready(m + 1)
            acc = acc + matmul(par, m + 1)
        ready(late)
        acc = acc + matmul(par, late)
        rate_forward(par, late).wait_recv()
        ready(late + 1)
        acc = acc + matmul(par, late + 1)
        if first:
            for m in range(1, split):
                sub_copy(it, m).wait_recv()

            @pl.when(it == 0)
            def _():
                load_recv.wait()

            summed = jnp.concatenate([subspace[it, j] for j in range(split)], 0).astype(jnp.bfloat16)
            base[...] = drive[...].astype(jnp.float32) + lax.dot_general(
                summed, w_rcv[...], TRANSPOSED, preferred_element_type=jnp.float32
            )
            acc = acc + base[...]
            for m in range(1, split):
                sub_copy(it, m).wait_send()

            @pl.loop(1, devices)
            def _(o):
                part_copy(it, o).wait_send()

        rate_copy(par, 1).wait_send()
        for m in forwarded:
            rate_copy(par, m).wait_send()
            rate_forward(par, m).wait_send()
        potential = voltage[...]
        potential = potential + leak[...] * (acc - potential)
        voltage[...] = potential
        firing = jnp.tanh(potential).astype(jnp.bfloat16)
        history[k] = firing
        rates[1 - par, 0] = firing

    @pl.loop(0, INTERVALS)
    def _(it):
        step(it, 0, True)

        @pl.loop(1, ticks)
        def _(k):
            step(it, k, False)


def body(
    devices, state_init, prior_interval_trace, drive_input, leak_rate, w_recur, w_send, w_recv,
    area_mask, coupling, delay_slot,
):
    ticks, trials, units = prior_interval_trace.shape
    rank = w_send.shape[1]
    split = w_recur.shape[1] // units
    areas = devices // split
    rows = trials // split
    vmem = pl.BlockSpec(memory_space=pltpu.VMEM)
    smem = pl.BlockSpec(memory_space=pltpu.SMEM)
    hbm = pl.BlockSpec(memory_space=pl.ANY)
    dma = pltpu.SemaphoreType.DMA
    return pl.pallas_call(
        functools.partial(kernel, devices, split),
        out_shape=(
            jax.ShapeDtypeStruct(state_init.shape, jnp.float32),
            jax.ShapeDtypeStruct(prior_interval_trace.shape, jnp.bfloat16),
        ),
        in_specs=[vmem, vmem, vmem, vmem, hbm, hbm, hbm, smem, smem, smem],
        out_specs=(vmem, vmem),
        scratch_shapes=[
            pltpu.VMEM((split, units, units), jnp.bfloat16),
            pltpu.VMEM((units, rank), jnp.bfloat16),
            pltpu.VMEM((units, rank), jnp.bfloat16),
            pltpu.VMEM((2, split, trials, units), jnp.bfloat16),
            pltpu.VMEM((ticks, trials, rank), jnp.float32),
            pltpu.VMEM((areas, split, rows, rank), jnp.float32),
            pltpu.VMEM((INTERVALS, devices, rows, rank), jnp.float32),
            pltpu.VMEM((INTERVALS, split, rows, rank), jnp.float32),
            pltpu.VMEM((trials, units), jnp.float32),
            dma((split + 2,)),
            dma((split,)),
            dma((split,)),
            dma((2, split)),
            dma((devices,)),
            dma((INTERVALS, devices)),
            dma((split,)),
            dma((INTERVALS, split)),
        ],
        compiler_params=pltpu.CompilerParams(
            collective_id=0, has_side_effects=True, vmem_limit_bytes=48 * 1024 * 1024
        ),
    )(
        state_init, prior_interval_trace, drive_input, leak_rate.reshape(1, units),
        w_recur, w_send, w_recv, area_mask, coupling, delay_slot,
    )


def solution(mesh):
    in_specs = (
        P("group", "area"),
        P(None, "group", "area"),
        P("group", "area"),
        P(("group", "area")),
        P(("group", "area"), None),
        P(("group", "area"), None),
        P(("group", "area"), None),
        P("group", None),
        P("group", None),
        P("group", None),
    )
    out_specs = (P("group", "area"), P(None, "group", "area"))
    return jax.shard_map(
        functools.partial(body, mesh.shape["area"]),
        mesh=mesh, in_specs=in_specs, out_specs=out_specs, check_vma=False,
    )
```

time: 157 us -> 82.9 us (0.53)
  waiting for transfers between devices: 89.8 us -> 0 us
  Pallas kernels: 0 us -> 72.7 us
  matrix products: 33 us -> 0 us
  starting transfers between devices: 28.4 us -> 0 us
  local copies, waits for them, and re-layouts: 1.91 us -> 9.2 us
  other arithmetic: 2.62 us -> 0 us
    ppermute x32 -> x0, waiting for transfers between devices: 89.8 us -> none  [from_partner(): return lax.ppermute(block, axis, route)]
    pallas_call x0 -> x1, Pallas kernels: none -> 72.7 us  [body(): pl.pallas_call(functools.partial(kernel, devices, split), out_shape=(jax....]
    dot_general x14 -> x0, matrix products: 33 us -> none  [the longest x8 27.1 us: body(): lax.dot_general(gathered_activity, w_recur, (((1,), (1,)), ((), ())), pre...]
    ppermute x32 -> x0, starting transfers between devices: 28.4 us -> none  [from_partner(): return lax.ppermute(block, axis, route)]
    unnamed x14 -> x18, local copies, waits for them, and re-layouts: 0.06 us -> 8.51 us
  transfers between devices with their start and end apart: 32 -> 0, of which waited for: 29 -> 0; matrix products, arithmetic and copies ran while one was open for 2% -> 0% of each run, Pallas kernels for 0% -> 0%
where the time goes in v1:
time: 82.9 us; the launch traced here: 82.5 us
  Pallas kernels  72.7 us (88%)
  local copies, waits for them, and re-layouts  9.2 us (11%)
    pallas_call x1, Pallas kernels, body(): pl.pallas_call(functools.partial(kernel, devices, split), out_shape=(jax....  72.7 us
    unnamed x18, local copies, waits for them, and re-layouts  8.51 us

profile of v1, /device:TPU:0, one launch (start us, length us, event | category | flops | bytes accessed | tf_op | source)
XLA Modules:
  0.0 82.5 jit_solution(5133441425925118149)
XLA Ops:
  0.6 0.7 reshape.7.leak
  1.3 0.0 copy-start
  1.3 1.3 %copy-done = bf16[768,768]{1,0:T(8,128)(2,1)S(1)} copy-done((bf16[768,768]{1,0:T(8,128)(2,1)S(1)}, bf16[768,768]{1,0:T(8,128)(2,1)}, u32[]{:S(2)}) %copy-start) | copy-done | bytes 1179672
  2.6 0.0 copy-start.1
  2.6 1.3 %copy-done.1 = bf16[768,768]{1,0:T(8,128)(2,1)S(1)} copy-done((bf16[768,768]{1,0:T(8,128)(2,1)S(1)}, bf16[768,768]{1,0:T(8,128)(2,1)}, u32[]{:S(2)}) %copy-start.1) | copy-done | bytes 1179672
  3.9 0.0 copy-start.2
  3.9 0.9 %copy-done.2 = bf16[4,32,768]{2,1,0:T(8,128)(2,1)S(1)} copy-done((bf16[4,32,768]{2,1,0:T(8,128)(2,1)S(1)}, bf16[4,32,768]{2,1,0:T(8,128)(2,1)}, u32[]{:S(2)}) %copy-start.2) | copy-done | bytes 196632
  4.8 0.0 copy-start.3
  4.8 0.9 %copy-done.3 = f32[32,768]{1,0:T(8,128)S(1)} copy-done((f32[32,768]{1,0:T(8,128)S(1)}, f32[32,768]{1,0:T(8,128)}, u32[]{:S(2)}) %copy-start.3) | copy-done | bytes 98328
  5.7 0.0 copy-start.4
  5.7 0.8 copy-done.4
  6.5 0.0 copy-start.5
  6.5 0.7 copy-done.5
  7.2 0.0 copy-start.6
  7.2 0.7 copy-done.6
  7.8 0.0 copy-start.7
  7.8 0.7 copy-done.7
  8.5 72.7 %shard_map.113 = (f32[32,768]{1,0:T(8,128)S(1)}, bf16[4,32,768]{2,1,0:T(8,128)(2,1)S(1)}) custom-call(f32[32,768]{1,0:T(8,128)S(1)} %copy-done.3, bf16[4,32,768]{2,1,0:T(8,128)(2,1)S(1)} %copy-done.2, bf16[32,768]{1,0:T(8,128)(2,1)S(1)} %copy-done.4, f32[1,768]{1,0:T(1,128)S(1)} %reshape.7.leak, bf16[768,6144]{1,0:T(8,128)(2,1)} %w_recur.1, ...), custom_call_target="tpu_custom_call" | custom-call | tf_op jit(solution)/shard_map/pallas_call | solution.py:206
  81.2 0.6 copy.14
  81.8 0.7 copy.15
Async XLA Ops:
  1.3 1.3 %copy-start = (bf16[768,768]{1,0:T(8,128)(2,1)S(1)}, bf16[768,768]{1,0:T(8,128)(2,1)}, u32[]{:S(2)}) copy-start(bf16[768,768]{1,0:T(8,128)(2,1)} %w_send.1) | copy-start | bytes 3538948
  2.6 1.3 %copy-start.1 = (bf16[768,768]{1,0:T(8,128)(2,1)S(1)}, bf16[768,768]{1,0:T(8,128)(2,1)}, u32[]{:S(2)}) copy-start(bf16[768,768]{1,0:T(8,128)(2,1)} %w_recv.1) | copy-start | bytes 3538948
  3.9 0.9 %copy-start.2 = (bf16[4,32,768]{2,1,0:T(8,128)(2,1)S(1)}, bf16[4,32,768]{2,1,0:T(8,128)(2,1)}, u32[]{:S(2)}) copy-start(bf16[4,32,768]{2,1,0:T(8,128)(2,1)} %prior.1) | copy-start | bytes 589828
  4.8 0.9 %copy-start.3 = (f32[32,768]{1,0:T(8,128)S(1)}, f32[32,768]{1,0:T(8,128)}, u32[]{:S(2)}) copy-start(f32[32,768]{1,0:T(8,128)} %state.1) | copy-start | bytes 294916
  5.7 0.8 copy-start.4
  6.5 0.7 copy-start.5
  7.2 0.7 copy-start.6
  7.8 0.7 copy-start.7
